TPU v7x, 32 devices: a whole 2x2x4 slice. The times are simulated.
32 devices in a mesh: row: 8 (over z, x), col: 2 (over core), dp: 2 (over y).
Axes of the slice: x: 2, y: 2, z: 4, core: 2. Of those that a mesh axis runs over, the one named last changes fastest.
Arguments:
- pixels: bfloat16 [2, 3, 256, 256], P('dp', None, 'row', 'col'), may hold values from -6 to 6
- cotangent: bfloat16 [2, 64, 64, 1024], P('dp', 'row', 'col'), may hold values from -6 to 6
- embed_weight: bfloat16 [48, 1024], replicated, may hold values from -0.875 to 0.875
- embed_bias: float32 [1024], replicated, may hold values from -4 to 4
- layer_norm_gain: float32 [1024], replicated, may hold values from 0.5 to 1.5
- qkv_weight: bfloat16 [1024, 2304], P('row', ('col', 'dp')), may hold values from -0.1875 to 0.1875
- out_weight: bfloat16 [768, 1024], P('row', ('col', 'dp')), may hold values from -0.21875 to 0.21875
- bias_table: float32 [12, 225], replicated, may hold values from -4 to 404
- rel_index: int32 [64, 64], replicated, may hold values from 0 to 224
- shifts: int32 [2, 2], P('dp'), may hold values from 1 to 7
Outputs:
- out_weight_grad: float32 [768, 1024], P('row', ('col', 'dp'))
- embed_weight_grad: float32 [48, 1024], replicated
- embed_bias_grad: float32 [1024], replicated
- norm_gain_grad: float32 [1024], replicated
- bias_table_grad: float32 [12, 225], replicated
Inputs may be any that keep to these rules, and one draw needn't show every extreme that they name: `rel_index`: each entry names one of the 225 columns of bias_table.
All inputs are finite; a program needn't handle non-finite values.
Results may differ from a plain program's by a relative error of at most 0.023.
Values may be sent and summed in bfloat16 or wider, within the bound.
A program may use at most 64 MiB of HBM per device.

v0:
```python
import jax
import jax.numpy as jnp
from jax import lax
from jax.sharding import PartitionSpec as P

WIN = 8
PATCH = 4
norm_epsilon = 1e-05


def from_behind(value, axis, steps):
    count = lax.axis_size(axis)
    pairs = [(source, (source + steps) % count) for source in range(count)]
    return lax.ppermute(value, axis, pairs)


def make_patches(pixel_block):
    images, channels, pixel_rows, pixel_cols = pixel_block.shape
    grid_rows = pixel_rows // PATCH
    grid_cols = pixel_cols // PATCH
    shaped = pixel_block.reshape(images, channels, grid_rows, PATCH, grid_cols, PATCH)
    return shaped.transpose(0, 2, 4, 1, 3, 5).reshape(
        images, grid_rows, grid_cols, channels * PATCH * PATCH
    )


def embed_cells(patches, embed_weight, embed_bias):
    return (jnp.dot(patches, embed_weight, preferred_element_type=jnp.float32) + embed_bias).astype(
        jnp.bfloat16
    )


def window_split(block):
    rows_all, cols_all, features = block.shape
    shaped = block.reshape(rows_all // WIN, WIN, cols_all // WIN, WIN, features)
    return shaped.transpose(0, 2, 1, 3, 4).reshape(-1, WIN * WIN, features)


def window_join(windows, rows_all, cols_all):
    features = windows.shape[-1]
    shaped = windows.reshape(rows_all // WIN, cols_all // WIN, WIN, WIN, features)
    return shaped.transpose(0, 2, 1, 3, 4).reshape(rows_all, cols_all, features)


def splice_after(own_block, borrowed, offsets, along_dim):
    length = own_block.shape[along_dim]

    def single(own_item, borrowed_item, offset):
        joined = jnp.concatenate([own_item, borrowed_item], along_dim - 1)
        return lax.dynamic_slice_in_dim(joined, offset, length, along_dim - 1)

    return jax.vmap(single)(own_block, borrowed, offsets)


def splice_before(own_block, borrowed, offsets, along_dim):
    length = own_block.shape[along_dim]
    margin = borrowed.shape[along_dim]

    def single(own_item, borrowed_item, offset):
        joined = jnp.concatenate([borrowed_item, own_item], along_dim - 1)
        return lax.dynamic_slice_in_dim(joined, margin - offset, length, along_dim - 1)

    return jax.vmap(single)(own_block, borrowed, offsets)


def attend_forward(cell_windows, labels, layer_norm_gain, qkv_full, bias_full):
    window_count, cell_count, features = cell_windows.shape
    head_count = bias_full.shape[0]
    inner_width = qkv_full.shape[1] // 3
    head_size = inner_width // head_count
    score_scale = head_size ** (-0.5)
    flat_rows = cell_windows.reshape(-1, features).astype(jnp.float32)
    average = jnp.mean(flat_rows, axis=-1, keepdims=True)
    centered_input = flat_rows - average
    inverse_deviation = lax.rsqrt(
        jnp.mean(centered_input * centered_input, axis=-1, keepdims=True) + norm_epsilon
    )
    standardized_rows = centered_input * inverse_deviation
    normalized_rows = (standardized_rows * layer_norm_gain).astype(jnp.bfloat16)
    projected = jnp.dot(normalized_rows, qkv_full, preferred_element_type=jnp.float32).astype(
        jnp.bfloat16
    )
    head_shape = (window_count, cell_count, head_count, head_size)
    query_rows = projected[:, :inner_width].reshape(head_shape)
    key_vectors = projected[:, inner_width : 2 * inner_width].reshape(head_shape)
    value_rows = projected[:, 2 * inner_width :].reshape(head_shape)
    scores = (
        jnp.einsum("wmhd,wnhd->whmn", query_rows, key_vectors, preferred_element_type=jnp.float32)
        * score_scale
        + bias_full[None]
    )
    same_region = labels[:, None, :, None] == labels[:, None, None, :]
    scores = jnp.where(same_region, scores, -1e30)
    row_peak = jnp.max(scores, axis=-1, keepdims=True)
    exp_scores = jnp.exp(scores - row_peak)
    attention_weights = exp_scores / jnp.sum(exp_scores, axis=-1, keepdims=True)
    reduced_probability = attention_weights.astype(jnp.bfloat16)
    attended = jnp.einsum(
        "whmn,wnhd->wmhd", reduced_probability, value_rows, preferred_element_type=jnp.float32
    ).astype(jnp.bfloat16)
    stored_residuals = (
        standardized_rows,
        inverse_deviation,
        query_rows,
        key_vectors,
        value_rows,
        attention_weights,
        reduced_probability,
    )
    return (stored_residuals, attended.reshape(-1, inner_width))


def attend_backward(stored_residuals, d_attended, layer_norm_gain, qkv_full):
    (
        standardized_rows,
        inverse_deviation,
        query_rows,
        key_vectors,
        value_rows,
        attention_weights,
        reduced_probability,
    ) = stored_residuals
    head_shape = query_rows.shape
    score_scale = head_shape[3] ** (-0.5)
    total_row_count = standardized_rows.shape[0]
    inner_width = head_shape[2] * head_shape[3]
    d_heads = d_attended.reshape(head_shape)
    d_prob = jnp.einsum("wmhd,wnhd->whmn", d_heads, value_rows, preferred_element_type=jnp.float32)
    d_values = jnp.einsum(
        "whmn,wmhd->wnhd", reduced_probability, d_heads, preferred_element_type=jnp.float32
    ).astype(jnp.bfloat16)
    d_scores = attention_weights * (
        d_prob - jnp.sum(attention_weights * d_prob, axis=-1, keepdims=True)
    )
    table_part = jnp.sum(d_scores, axis=0)
    d_low = d_scores.astype(jnp.bfloat16)
    d_queries = (
        jnp.einsum("whmn,wnhd->wmhd", d_low, key_vectors, preferred_element_type=jnp.float32)
        * score_scale
    ).astype(jnp.bfloat16)
    d_keys = (
        jnp.einsum("whmn,wmhd->wnhd", d_low, query_rows, preferred_element_type=jnp.float32)
        * score_scale
    ).astype(jnp.bfloat16)
    d_projected = jnp.concatenate(
        [
            d_queries.reshape(total_row_count, inner_width),
            d_keys.reshape(total_row_count, inner_width),
            d_values.reshape(total_row_count, inner_width),
        ],
        axis=1,
    )
    normalized_gradient = lax.dot_general(
        d_projected, qkv_full, (((1,), (1,)), ((), ())), preferred_element_type=jnp.float32
    )
    gain_contribution = jnp.sum(normalized_gradient * standardized_rows, axis=0)
    scaled_rows = normalized_gradient * layer_norm_gain
    branch_gradient = inverse_deviation * (
        scaled_rows
        - jnp.mean(scaled_rows, axis=-1, keepdims=True)
        - standardized_rows * jnp.mean(scaled_rows * standardized_rows, axis=-1, keepdims=True)
    )
    return (branch_gradient.astype(jnp.bfloat16), gain_contribution, table_part)


def on_device(
    pixels,
    cotangent,
    embed_weight,
    embed_bias,
    layer_norm_gain,
    qkv_weight,
    out_weight,
    bias_table,
    rel_index,
    shifts,
):
    images, rows_dev, cols_dev, features = cotangent.shape
    head_count = bias_table.shape[0]
    grid_rows = rows_dev * lax.axis_size("row")
    grid_cols = cols_dev * lax.axis_size("col")
    row_shift = shifts[:, 0]
    col_shift = shifts[:, 1]
    qkv_rowwise = lax.all_gather(qkv_weight, "row", axis=0, tiled=True)
    qkv_full, out_columns = (
        lax.all_gather(qkv_rowwise, ("col", "dp"), axis=1, tiled=True),
        lax.all_gather(out_weight, ("col", "dp"), axis=1, tiled=True),
    )
    patches = make_patches(pixels)
    tokens = embed_cells(patches, embed_weight, embed_bias)
    below = from_behind((tokens, cotangent), "row", -1)
    shifted = splice_after(tokens, below[0], row_shift, 1)
    shifted_cot = splice_after(cotangent, below[1], row_shift, 1)
    beside = from_behind((shifted[:, :, :WIN], shifted_cot[:, :, :WIN]), "col", -1)
    shifted = splice_after(shifted, beside[0], col_shift, 2)
    shifted_cot = splice_after(shifted_cot, beside[1], col_shift, 2)
    row_ids = lax.axis_index("row") * rows_dev + jnp.arange(rows_dev, dtype=jnp.int32)
    col_ids = lax.axis_index("col") * cols_dev + jnp.arange(cols_dev, dtype=jnp.int32)
    row_part = (row_ids[None, :] >= grid_rows - row_shift[:, None]).astype(jnp.int32)
    col_part = (col_ids[None, :] >= grid_cols - col_shift[:, None]).astype(jnp.int32)
    region = 2 * row_part[:, :, None] + col_part[:, None, :]
    labels = window_split(region.reshape(images * rows_dev, cols_dev, 1))[:, :, 0]
    cell_windows = window_split(shifted.reshape(images * rows_dev, cols_dev, features))
    cot_flat = window_split(shifted_cot.reshape(images * rows_dev, cols_dev, features)).reshape(
        -1, features
    )
    selector = (
        rel_index.reshape(-1)[:, None] == jnp.arange(bias_table.shape[1], dtype=jnp.int32)[None, :]
    ).astype(jnp.float32)
    bias_full = jnp.dot(selector, bias_table.T, precision=lax.Precision.HIGHEST).T.reshape(
        head_count, WIN * WIN, WIN * WIN
    )
    stored_residuals, attended = attend_forward(
        cell_windows, labels, layer_norm_gain, qkv_full, bias_full
    )
    d_attended = lax.dot_general(
        cot_flat,
        lax.all_gather(out_columns, "row", axis=0, tiled=True),
        (((1,), (1,)), ((), ())),
        preferred_element_type=jnp.float32,
    ).astype(jnp.bfloat16)
    partial_rows = lax.psum_scatter(
        lax.dot_general(
            attended, cot_flat, (((0,), (0,)), ((), ())), preferred_element_type=jnp.float32
        ),
        "row",
        scatter_dimension=0,
        tiled=True,
    )
    out_weight_grad = lax.psum_scatter(partial_rows, ("col", "dp"), scatter_dimension=1, tiled=True)
    d_rows, gain_contribution, table_part = attend_backward(
        stored_residuals, d_attended, layer_norm_gain, qkv_full
    )
    branch_gradient = window_join(
        d_rows.reshape(-1, WIN * WIN, features), images * rows_dev, cols_dev
    ).reshape(images, rows_dev, cols_dev, features)
    patch_rows = patches.reshape(-1, patches.shape[-1])
    cot_rows = cotangent.reshape(-1, features)
    contract = (((0,), (0,)), ((), ()))
    behind = from_behind(branch_gradient[:, :, cols_dev - WIN :], "col", 1)
    d_back = splice_before(branch_gradient, behind, col_shift, 2)
    above = from_behind(d_back, "row", 1)
    d_back = splice_before(d_back, above, row_shift, 1)
    back_rows = d_back.reshape(-1, features)
    embed_grad = lax.dot_general(
        patch_rows, cot_rows, contract, preferred_element_type=jnp.float32
    ) + lax.dot_general(patch_rows, back_rows, contract, preferred_element_type=jnp.float32)
    bias_grad = jnp.sum(cot_rows, axis=0, dtype=jnp.float32) + jnp.sum(
        back_rows, axis=0, dtype=jnp.float32
    )
    table_grad = jnp.dot(
        table_part.reshape(head_count, -1), selector, precision=lax.Precision.HIGHEST
    )
    totals = lax.psum((embed_grad, bias_grad, gain_contribution, table_grad), ("row", "col", "dp"))
    return (out_weight_grad, totals[0], totals[1], totals[2], totals[3])


def solution(mesh):
    return jax.shard_map(
        on_device,
        mesh=mesh,
        in_specs=(
            P("dp", None, "row", "col"),
            P("dp", "row", "col", None),
            P(),
            P(),
            P(),
            P("row", ("col", "dp")),
            P("row", ("col", "dp")),
            P(),
            P(),
            P("dp", None),
        ),
        out_specs=(P("row", ("col", "dp")), P(), P(), P(), P()),
        check_vma=False,
    )
```

profile of v0, /device:TPU:0, one launch (start us, length us, event | category | flops | bytes accessed | tf_op | source)
XLA Modules:
  0.0 390.5 jit_solution(13253919688802146951)
XLA Ops:
  7.2 0.7 all-gather.4.cloned.1.call-update
  8.0 45.2 %all-gather.4.cloned.1.call-done = bf16[1024,576]{0,1:T(8,128)(2,1)} async-done(((bf16[128,576]{0,1:T(8,128)(2,1)}), bf16[1024,576]{0,1:T(8,128)(2,1)}) %all-gather.4.cloned.1.call-update) | async-done | bytes 1179664 | tf_op jit(solution)/shard_map/all_gather | solution.py:184
  53.2 2.1 collective-permute-start.2
  55.4 2.4 reshape.177
  57.8 0.7 copy.154
  58.5 0.3 fusion.11
  58.8 1.2 collective-permute-start
  60.0 12.5 %all_gather.14 = bf16[96,1024]{1,0:T(8,128)(2,1)} all-gather(bf16[96,256]{1,0:T(8,128)(2,1)S(1)} %copy-done.13), channel_id=1, replica_groups=mesh['row'=8,'col'=2,'dp'=2] {'col','dp'}, dimensions={1}, use_global_device_ids=true | all-gather | bytes 245760 | tf_op jit(solution)/shard_map/all_gather | solution.py:187
  72.6 0.6 fusion.44
  76.8 2.6 convolution_bitcast_fusion
  79.4 0.2 fusion.32
  81.3 0.9 copy.165
  82.9 0.2 fusion.31
  83.1 0.6 collective-permute-start.3
  83.7 0.4 fusion.42
  84.2 0.5 collective-permute-done.3
  84.6 0.3 fusion.27
  84.9 0.8 copy.169
  85.9 0.3 multiply_reduce_fusion.3
  86.2 0.2 copy-done.15
  86.5 0.2 multiply_convert_fusion.3
  86.7 7.0 %all-gather.6.cloned.1.call-done = bf16[1024,2304]{0,1:T(8,128)(2,1)} async-done(((bf16[1024,576]{0,1:T(8,128)(2,1)}), bf16[1024,2304]{0,1:T(8,128)(2,1)}) %all-gather.6.cloned.1.call-update) | async-done | bytes 4718608 | tf_op jit(solution)/shard_map/all_gather | solution.py:186
  93.7 3.8 convolution_convert_fusion
  97.5 1.0 fusion.43
  98.4 0.6 reshape.368
  99.1 0.9 copy.174
  99.9 2.5 reshape.366
  102.5 1.6 reshape.367
  104.1 1.8 copy.178
  105.9 1.4 add_select_fusion
  107.3 1.6 fusion.45
  109.0 3.8 fusion.7
  112.7 2.7 copy.168
  115.4 2.5 reshape.182
  117.9 3.4 fusion.46
  121.3 0.2 all-reduce.5.cloned.1.call-start
  121.5 17.9 %all-gather.8.cloned.1.call-done = bf16[768,1024]{1,0:T(8,128)(2,1)} async-done(((bf16[96,1024]{1,0:T(8,128)(2,1)}), bf16[768,1024]{1,0:T(8,128)(2,1)}) %all-gather.8.cloned.1.call-update) | async-done | bytes 1572880 | tf_op jit(solution)/shard_map/all_gather | solution.py:218
  139.4 3.0 convolution_convert_fusion.3
  142.4 2.4 reshape.369
  144.8 2.5 copy.182
  147.3 2.8 multiply_reduce_fusion
  150.1 1.3 fusion.20
  151.4 0.9 copy-done.1
  152.3 1.5 fusion.9
  153.8 2.3 copy.177
  156.0 2.5 reshape.185
  158.5 1.4 fusion.10
  160.0 1.6 copy.181
  161.6 1.2 reshape.186
  162.8 3.5 fusion.8
  166.3 1.8 copy.184
  168.1 1.2 reshape.187
  169.3 4.2 %multiply_reduce_fusion.1 = (f32[1024]{0:T(1024)S(1)}, f32[256]{0:T(256)S(1)}, f32[256]{0:T(256)S(1)}, f32[256,1024]{1,0:T(8,128)S(1)}) fusion(f32[1,4,8,8,1024]{4,3,2,1,0:T(8,128)S(1)} %copy.156, f32[256]{0:T(256)S(1)} %rsqrt.12, f32[256]{0:T(256)S(1)} %div.23, f32[1024]{0:T(1024)S(1)} %copy-done.15, bf16[1024,2304]{0,1:T(8,128)(2,1)} %all-gather.6.cloned.1.call-done, ...), kind=kOutput, calls=%fused_computation.41 | convolution fusion | flops 1213594112 | bytes 8007680 | tf_op jit(solution)/shard_map/dot_general | solution.py:153
  173.5 0.3 multiply_convert_fusion.2
  175.6 0.4 collective-permute-start.5
  177.6 15.2 %collective-permute-done.5 = bf16[1,8,32,1024]{3,2,1,0:T(8,128)(2,1)S(1)} collective-permute-done((bf16[1,8,32,1024]{3,2,1,0:T(8,128)(2,1)S(1)}, bf16[1,8,32,1024]{3,2,1,0:T(8,128)(2,1)S(1)}, u32[]{:S(2)}, u32[]{:S(2)}) %collective-permute-start.5) | collective-permute-done | bytes 524320 | tf_op jit(solution)/shard_map/ppermute | solution.py:14
  192.7 0.3 convert_reduce_fusion
  193.0 0.9 fusion.18
  194.0 33.6 %reduce-scatter.3.cloned.1.call-done = f32[96,1024]{1,0:T(8,128)} async-done(((f32[768,1024]{1,0:T(8,128)}), f32[96,1024]{1,0:T(8,128)}) %reduce-scatter.3.cloned.1.call-update) | async-done | bytes 393232 | tf_op jit(solution)/shard_map/reduce_scatter | solution.py:222
  228.1 1.4 fusion.1
  229.5 40.2 %all-reduce.2 = (f32[1024]{0:T(1024)}, f32[1024]{0:T(1024)}, f32[12,225]{1,0:T(8,128)}) all-reduce(f32[1024]{0:T(1024)S(1)} %add.134, f32[1024]{0:T(1024)S(1)} %get-tuple-element.71, f32[12,225]{1,0:T(8,128)S(1)} %fusion.1), channel_id=1, replica_groups=mesh['row'=8,'col'=2,'dp'=2] {'row','col','dp'}, use_global_device_ids=true, to_apply=%region_12.13 | all-reduce | flops 4748 | bytes 37984 | tf_op jit(solution)/shard_map/psum | solution.py:254
  269.7 87.6 %all-reduce.5.cloned.1.call-done = f32[48,1024]{1,0:T(8,128)} async-done(((f32[48,1024]{1,0:T(8,128)}), f32[48,1024]{1,0:T(8,128)}) %all-reduce.5.cloned.1.call-update) | async-done | bytes 196624 | tf_op jit(solution)/shard_map/psum | solution.py:254
  357.4 24.7 %reduce-scatter.5.cloned.1.call-done = f32[96,256]{1,0:T(8,128)} async-done(((f32[96,1024]{1,0:T(8,128)}), f32[96,256]{1,0:T(8,128)}) %reduce-scatter.5.cloned.1.call-update) | async-done | bytes 98320 | tf_op jit(solution)/shard_map/reduce_scatter | solution.py:230
  382.1 1.6 copy.218
  (81 shorter events, 2.4 us)
Async XLA Ops:
  7.2 51.3 %copy-start = (bf16[48,1024]{1,0:T(8,128)(2,1)S(1)}, bf16[48,1024]{1,0:T(8,128)(2,1)}, u32[]{:S(2)}) copy-start(bf16[48,1024]{1,0:T(8,128)(2,1)} %param.12) | copy-start | bytes 294916
  7.2 51.3 %copy-start.18 = (f32[1024]{0:T(1024)S(1)}, f32[1024]{0:T(1024)}, u32[]{:S(2)}) copy-start(f32[1024]{0:T(1024)} %param.13) | copy-start | bytes 12292
  7.2 45.9 %all-gather.4.cloned.1.call-start = ((), (), s32[]{:S(2)}) async-start(), calls=%async_computation.2 | async-start | bytes 1327104 | tf_op jit(solution)/shard_map/all_gather | solution.py:184
  7.9 85.8 %all-gather.6.cloned.1.call-start = ((), (), s32[]{:S(2)}) async-start(), calls=%async_computation.3 | async-start | bytes 5898240 | tf_op jit(solution)/shard_map/all_gather | solution.py:186
  53.1 6.9 %copy-start.13 = (bf16[96,256]{1,0:T(8,128)(2,1)S(1)}, bf16[96,256]{1,0:T(8,128)(2,1)}, u32[]{:S(2)}) copy-start(bf16[96,256]{1,0:T(8,128)(2,1)} %param.16) | copy-start | bytes 147460
  53.2 19.5 %copy-start.19 = (s32[1,2]{1,0:T(1,128)S(1)}, s32[1,2]{1,0:T(1,128)}, u32[]{:S(2)}) copy-start(s32[1,2]{1,0:T(1,128)} %param.19) | copy-start | bytes 28
  53.2 22.8 %copy-start.14 = (s32[64,64]{1,0:T(8,128)S(1)}, s32[64,64]{1,0:T(8,128)}, u32[]{:S(2)}) copy-start(s32[64,64]{1,0:T(8,128)} %param.18) | copy-start | bytes 49156
  53.2 23.6 %copy-start.20 = (f32[12,225]{1,0:T(8,128)S(1)}, f32[12,225]{1,0:T(8,128)}, u32[]{:S(2)}) copy-start(f32[12,225]{1,0:T(8,128)} %param.17) | copy-start | bytes 32404
  53.2 86.2 %all-gather.8.cloned.1.call-start = ((), (), s32[]{:S(2)}) async-start(), calls=%async_computation.6 | async-start | bytes 1769472 | tf_op jit(solution)/shard_map/all_gather | solution.py:218
  53.2 29.6 %collective-permute-start.2 = (bf16[1,8,32,1024]{3,2,1,0:T(8,128)(2,1)}, bf16[1,8,32,1024]{3,2,1,0:T(8,128)(2,1)S(1)}, u32[]{:S(2)}, u32[]{:S(2)}) collective-permute-start(bf16[1,8,32,1024]{3,2,1,0:T(8,128)(2,1)} %param.11), channel_id=1, source_target_pairs={{0,28},{4,0},{8,4},{12,8},{16,12},{20,16},{24,20},{28,24},{1,29},{... | collective-permute-start | bytes 1572872 | tf_op jit(solution)/shard_map/ppermute | solution.py:14
  58.5 20.9 %copy-start.8 = (bf16[1,8,32,3,4,4]{2,1,5,4,3,0:T(8,128)(2,1)}, bf16[1,8,32,3,4,4]{2,1,5,4,3,0:T(8,128)(2,1)S(1)}, u32[]{:S(2)}) copy-start(bf16[1,8,32,3,4,4]{2,1,5,4,3,0:T(8,128)(2,1)S(1)} %copy.154) | copy-start | bytes 73732
  58.8 20.5 %collective-permute-start = (bf16[1,8,32,1024]{3,2,1,0:T(8,128)(2,1)S(1)}, bf16[1,8,32,1024]{3,2,1,0:T(8,128)(2,1)S(1)}, u32[]{:S(2)}, u32[]{:S(2)}) collective-permute-start(bf16[1,8,32,1024]{3,2,1,0:T(8,128)(2,1)S(1)} %fusion.11), channel_id=1, source_target_pairs={{0,28},{4,0},{8,4},{12,8},{16,12},{20,16},{24,20},{28,24},{1,29},{... | collective-permute-start | bytes 1572872 | tf_op jit(solution)/shard_map/ppermute | solution.py:14
  72.6 155.0 %reduce-scatter.3.cloned.1.call-start = ((), (), s32[]{:S(2)}) async-start(), calls=%async_computation.4 | async-start | bytes 3538944 | tf_op jit(solution)/shard_map/reduce_scatter | solution.py:222
  76.1 3.3 copy-start.16
  79.4 3.5 copy-start.5
  79.6 4.0 %collective-permute-start.1 = (bf16[1,8,8,1024]{3,2,1,0:T(8,128)(2,1)S(1)}, bf16[1,8,8,1024]{3,2,1,0:T(8,128)(2,1)S(1)}, u32[]{:S(2)}, u32[]{:S(2)}) collective-permute-start(bf16[1,8,8,1024]{3,2,1,0:T(8,128)(2,1)S(1)} %slice.150), channel_id=1, source_target_pairs={{0,2},{2,0},{1,3},{3,1},{4,6},{6,4},{5,7},{7,5},{8,10},{10,8},{9,1... | collective-permute-start | bytes 393224 | tf_op jit(solution)/shard_map/ppermute | solution.py:14
  83.1 1.5 collective-permute-start.3
  85.8 0.7 copy-start.15
  99.9 2.6 copy-start.7
  107.3 1.6 copy-start.3
  121.3 236.1 %all-reduce.5.cloned.1.call-start = ((), (), s32[]{:S(2)}) async-start(), calls=%async_computation.7 | async-start | bytes 393216 | tf_op jit(solution)/shard_map/psum | solution.py:254
  147.3 2.8 copy-start.4
  151.4 0.9 copy-start.1
  153.8 4.8 %copy-start.2 = (bf16[4,12,64,64]{2,3,1,0:T(8,128)(2,1)S(1)}, bf16[4,12,64,64]{2,3,1,0:T(8,128)(2,1)}, u32[]{:S(2)}) copy-start(bf16[4,12,64,64]{2,3,1,0:T(8,128)(2,1)} %copy-done.1) | copy-start | bytes 1179652
  160.0 2.9 copy-start.10
  166.3 3.1 copy-start.11
  166.3 3.1 copy-start.12
  173.9 2.7 copy-start.9
  174.0 1.4 collective-permute-start.4
  175.6 17.2 %collective-permute-start.5 = (bf16[1,8,32,1024]{3,2,1,0:T(8,128)(2,1)S(1)}, bf16[1,8,32,1024]{3,2,1,0:T(8,128)(2,1)S(1)}, u32[]{:S(2)}, u32[]{:S(2)}) collective-permute-start(bf16[1,8,32,1024]{3,2,1,0:T(8,128)(2,1)S(1)} %fusion.25), channel_id=1, source_target_pairs={{0,4},{4,8},{8,12},{12,16},{16,20},{20,24},{24,28},{28,0},{1,5},{5... | collective-permute-start | bytes 1572872 | tf_op jit(solution)/shard_map/ppermute | solution.py:14
  192.7 35.0 %copy-start.6 = (f32[12,64,64]{1,2,0:T(8,128)S(1)}, f32[12,64,64]{1,2,0:T(8,128)}, u32[]{:S(2)}) copy-start(f32[12,64,64]{1,2,0:T(8,128)} %get-tuple-element.81) | copy-start | bytes 589828
  193.0 35.0 %copy-start.17 = (s32[4096]{0:T(1024)S(1)}, s32[4096]{0:T(1024)}, u32[]{:S(2)}) copy-start(s32[4096]{0:T(1024)} %copy-done.16) | copy-start | bytes 49156
  193.9 188.1 %reduce-scatter.5.cloned.1.call-start = ((), (), s32[]{:S(2)}) async-start(), calls=%async_computation.5 | async-start | bytes 491520 | tf_op jit(solution)/shard_map/reduce_scatter | solution.py:230
Sparse Core Ops, SparseCore 0:
  10.0 43.0 all-gather.3
  54.7 38.9 all-gather.5
  95.9 43.4 all-gather.7
  142.9 84.6 reduce-scatter.2
  233.6 123.7 all-reduce.4
  360.3 21.7 reduce-scatter.4
where the time goes:
time: 391 us
  waiting for transfers between devices  233 us (60%)
  blocking collectives  52.7 us (13%)
  local copies, waits for them, and re-layouts  38.4 us (10%)
  matrix products  34.1 us (9%)
  between operations  22.4 us (6%)
  other arithmetic  5.59 us (1%)
  starting transfers between devices  4.81 us (1%)
    psum x1, waiting for transfers between devices, on_device(): lax.psum((embed_grad, bias_grad, gain_contribution, table_grad), ('row',...  87.6 us
    all_gather x1, waiting for transfers between devices, on_device(): qkv_rowwise = lax.all_gather(qkv_weight, 'row', axis=0, tiled=True)  45.2 us
    psum x1, blocking collectives, on_device(): lax.psum((embed_grad, bias_grad, gain_contribution, table_grad), ('row',...  40.2 us
    reduce_scatter x1, waiting for transfers between devices, on_device(): lax.psum_scatter(lax.dot_general(attended, cot_flat, (((0,), (0,)), ((),...  33.6 us
    reduce_scatter x1, waiting for transfers between devices, on_device(): lax.psum_scatter(partial_rows, ('col', 'dp'), scatter_dimension=1, tiled=...  24.7 us
    all_gather x1, waiting for transfers between devices, on_device(): lax.all_gather(out_columns, 'row', axis=0, tiled=True)  17.9 us
    ppermute x6, waiting for transfers between devices, from_behind(): return lax.ppermute(value, axis, pairs)  15.7 us
    all_gather x1, blocking collectives, on_device(): lax.all_gather(out_weight, ('col', 'dp'), axis=1, tiled=True)  12.5 us
  transfers between devices with their start and end apart: 12, of which 8 were waited for; matrix products, arithmetic and copies ran while one was open for 19% of the time, Pallas kernels for 0%

commit v1 on v0

--- a/solution.py
+++ b/solution.py
@@ -251,7 +251,15 @@
     table_grad = jnp.dot(
         table_part.reshape(head_count, -1), selector, precision=lax.Precision.HIGHEST
     )
-    totals = lax.psum((embed_grad, bias_grad, gain_contribution, table_grad), ("row", "col", "dp"))
+
+    def _report_samples_all(a0):
+        across = "row"
+        which_axis = ("col", "dp")
+        for dev in (which_axis, across):
+            a0 = lax.psum(a0, dev)
+        return a0
+
+    totals = _report_samples_all((embed_grad, bias_grad, gain_contribution, table_grad))
     return (out_weight_grad, totals[0], totals[1], totals[2], totals[3])
 
 

time: 391 us -> 414 us (1.059)
  waiting for transfers between devices: 233 us -> 257 us
  local copies, waits for them, and re-layouts: 38.4 us -> 26.7 us
  blocking collectives: 52.7 us -> 62.2 us
    reduce_scatter x1, waiting for transfers between devices: 33.6 us -> 77.7 us  [on_device(): lax.psum_scatter(lax.dot_general(attended, cot_flat, (((0,), (0,)), ((),...]
    psum x1 -> x2, waiting for transfers between devices: 87.6 us -> 49.4 us  [_report_samples_all(): a0 = lax.psum(a0, dev)]
    all_gather x1, waiting for transfers between devices: 7.04 us -> 31.3 us  [on_device(): lax.all_gather(qkv_rowwise, ('col', 'dp'), axis=1, tiled=True)]
    all_gather x1, waiting for transfers between devices: 45.2 us -> 31.7 us  [on_device(): qkv_rowwise = lax.all_gather(qkv_weight, 'row', axis=0, tiled=True)]
    ppermute x6, waiting for transfers between devices: 15.7 us -> 25.1 us  [from_behind(): return lax.ppermute(value, axis, pairs)]
    psum x1 -> x2, blocking collectives: 40.2 us -> 48.8 us  [_report_samples_all(): a0 = lax.psum(a0, dev)]
  transfers between devices with their start and end apart: 12 -> 13, of which waited for: 8 -> 10; matrix products, arithmetic and copies ran while one was open for 19% -> 6% of each run, Pallas kernels for 0% -> 0%
where the time goes in v1:
time: 414 us
  waiting for transfers between devices  257 us (62%)
  blocking collectives  62.2 us (15%)
  matrix products  32.4 us (8%)
  local copies, waits for them, and re-layouts  26.7 us (6%)
  between operations  22.4 us (5%)
  other arithmetic  7.36 us (2%)
  starting transfers between devices  6.07 us (1%)
    reduce_scatter x1, waiting for transfers between devices, on_device(): lax.psum_scatter(lax.dot_general(attended, cot_flat, (((0,), (0,)), ((),...  77.7 us
    psum x2, waiting for transfers between devices, _report_samples_all(): a0 = lax.psum(a0, dev)  49.4 us
    psum x2, blocking collectives, _report_samples_all(): a0 = lax.psum(a0, dev)  48.8 us
    all_gather x1, waiting for transfers between devices, on_device(): qkv_rowwise = lax.all_gather(qkv_weight, 'row', axis=0, tiled=True)  31.7 us
    all_gather x1, waiting for transfers between devices, on_device(): lax.all_gather(qkv_rowwise, ('col', 'dp'), axis=1, tiled=True)  31.3 us
    ppermute x6, waiting for transfers between devices, from_behind(): return lax.ppermute(value, axis, pairs)  25.1 us
    reduce_scatter x1, waiting for transfers between devices, on_device(): lax.psum_scatter(partial_rows, ('col', 'dp'), scatter_dimension=1, tiled=...  23 us
    all_gather x1, waiting for transfers between devices, on_device(): lax.all_gather(out_columns, 'row', axis=0, tiled=True)  17.7 us
  transfers between devices with their start and end apart: 13, of which 10 were waited for; matrix products, arithmetic and copies ran while one was open for 6% of the time, Pallas kernels for 0%

profile of v1, /device:TPU:0, one launch (start us, length us, event | category | flops | bytes accessed | tf_op | source)
XLA Modules:
  0.0 413.8 jit_solution(13650641040560871555)
XLA Ops:
  7.2 0.7 all-gather.4.cloned.1.call-update
  8.0 13.4 %all_gather.14 = bf16[96,1024]{1,0:T(8,128)(2,1)} all-gather(bf16[96,256]{1,0:T(8,128)(2,1)} %param.16), channel_id=1, replica_groups=mesh['row'=8,'col'=2,'dp'=2] {'col','dp'}, dimensions={1}, use_global_device_ids=true | all-gather | bytes 245760 | tf_op jit(solution)/shard_map/all_gather | solution.py:187
  21.5 31.7 %all-gather.4.cloned.1.call-done = bf16[1024,576]{0,1:T(8,128)(2,1)} async-done(((bf16[128,576]{0,1:T(8,128)(2,1)}), bf16[1024,576]{0,1:T(8,128)(2,1)}) %all-gather.4.cloned.1.call-update) | async-done | bytes 1179664 | tf_op jit(solution)/shard_map/all_gather | solution.py:184
  53.2 2.1 collective-permute-start.2
  55.4 1.7 reshape.177
  57.1 0.7 copy.154
  57.8 0.3 fusion.11
  58.1 1.2 collective-permute-start
  59.3 0.6 fusion.44
  63.4 2.6 convolution_bitcast_fusion
  66.0 16.5 %collective-permute-done = bf16[1,8,32,1024]{3,2,1,0:T(8,128)(2,1)S(1)} collective-permute-done((bf16[1,8,32,1024]{3,2,1,0:T(8,128)(2,1)S(1)}, bf16[1,8,32,1024]{3,2,1,0:T(8,128)(2,1)S(1)}, u32[]{:S(2)}, u32[]{:S(2)}) %collective-permute-start) | collective-permute-done | bytes 524320 | tf_op jit(solution)/shard_map/ppermute | solution.py:14
  84.4 0.9 copy.165
  85.9 0.2 fusion.31
  86.2 0.6 collective-permute-start.3
  86.7 0.4 fusion.42
  87.2 0.5 collective-permute-done.3
  87.7 0.3 fusion.27
  88.2 0.3 multiply_reduce_fusion.3
  88.6 0.2 copy-done.16
  88.8 1.0 multiply_convert_fusion.3
  89.8 17.7 %all-gather.8.cloned.1.call-done = bf16[768,1024]{1,0:T(8,128)(2,1)} async-done(((bf16[96,1024]{1,0:T(8,128)(2,1)}), bf16[768,1024]{1,0:T(8,128)(2,1)}) %all-gather.8.cloned.1.call-update) | async-done | bytes 1572880 | tf_op jit(solution)/shard_map/all_gather | solution.py:218
  107.5 2.8 convolution_convert_fusion.3
  110.2 1.7 reshape.369
  112.0 1.6 copy.182
  113.5 31.3 %all-gather.6.cloned.1.call-done = bf16[1024,2304]{0,1:T(8,128)(2,1)} async-done(((bf16[1024,576]{0,1:T(8,128)(2,1)}), bf16[1024,2304]{0,1:T(8,128)(2,1)}) %all-gather.6.cloned.1.call-update) | async-done | bytes 4718608 | tf_op jit(solution)/shard_map/all_gather | solution.py:186
  144.9 3.8 convolution_convert_fusion
  148.6 0.9 fusion.43
  149.6 0.6 reshape.368
  150.2 0.9 copy.174
  151.1 2.6 reshape.366
  153.7 1.6 reshape.367
  155.3 1.8 copy.178
  157.1 1.4 add_select_fusion
  158.6 1.7 fusion.45
  160.2 3.6 fusion.8
  163.8 2.6 multiply_reduce_fusion
  166.3 1.3 fusion.20
  167.6 1.5 fusion.10
  169.1 1.5 fusion.9
  170.6 1.8 copy.177
  172.3 1.2 reshape.185
  173.6 0.6 copy.181
  174.2 1.2 reshape.186
  175.4 0.6 copy.184
  176.0 0.5 reshape.187
  176.5 4.2 %multiply_reduce_fusion.1 = (f32[1024]{0:T(1024)S(1)}, f32[256]{0:T(256)S(1)}, f32[256]{0:T(256)S(1)}, f32[256,1024]{1,0:T(8,128)S(1)}) fusion(f32[1,4,8,8,1024]{4,3,2,1,0:T(8,128)S(1)} %copy.156, f32[256]{0:T(256)S(1)} %rsqrt.12, f32[256]{0:T(256)S(1)} %div.23, f32[1024]{0:T(1024)S(1)} %copy-done.16, bf16[1024,2304]{0,1:T(8,128)(2,1)} %all-gather.6.cloned.1.call-done, ...), kind=kOutput, calls=%fused_computation.41 | convolution fusion | flops 1213594112 | bytes 8007680 | tf_op jit(solution)/shard_map/dot_general | solution.py:153
  180.8 0.3 multiply_convert_fusion.2
  181.2 0.3 collective-permute-start.4
  183.0 1.5 collective-permute-start.5
  186.2 3.5 fusion.7
  189.7 1.8 copy.168
  191.4 0.5 reshape.182
  191.9 8.1 %collective-permute-done.5 = bf16[1,8,32,1024]{3,2,1,0:T(8,128)(2,1)} collective-permute-done((bf16[1,8,32,1024]{3,2,1,0:T(8,128)(2,1)S(1)}, bf16[1,8,32,1024]{3,2,1,0:T(8,128)(2,1)}, u32[]{:S(2)}, u32[]{:S(2)}) %collective-permute-start.5) | collective-permute-done | bytes 524320 | tf_op jit(solution)/shard_map/ppermute | solution.py:14
  200.0 1.2 convert_reduce_fusion
  201.2 0.9 fusion.18
  202.2 2.2 fusion.46
  204.5 27.1 %all-reduce.7.cloned.1.call-done = f32[48,1024]{1,0:T(8,128)} async-done(((f32[48,1024]{1,0:T(8,128)}), f32[48,1024]{1,0:T(8,128)}) %all-reduce.7.cloned.1.call-update) | async-done | bytes 196624 | tf_op jit(solution)/shard_map/psum | solution.py:259
  231.7 77.7 %reduce-scatter.3.cloned.1.call-done = f32[96,1024]{1,0:T(8,128)} async-done(((f32[768,1024]{1,0:T(8,128)}), f32[96,1024]{1,0:T(8,128)}) %reduce-scatter.3.cloned.1.call-update) | async-done | bytes 393232 | tf_op jit(solution)/shard_map/reduce_scatter | solution.py:222
  309.8 1.4 fusion.1
  311.3 12.8 %all-reduce.3 = (f32[1024]{0:T(1024)S(1)}, f32[1024]{0:T(1024)S(1)}, f32[12,225]{1,0:T(8,128)S(1)}) all-reduce(f32[1024]{0:T(1024)S(1)} %add.142, f32[1024]{0:T(1024)S(1)} %get-tuple-element.71, f32[12,225]{1,0:T(8,128)S(1)} %fusion.1), channel_id=1, replica_groups=mesh['row'=8,'col'=2,'dp'=2] {'col','dp'}, use_global_device_ids=true, to_apply=%region_13.14 | all-reduce | flops 4748 | bytes 37984 | tf_op jit(solution)/shard_map/psum | solution.py:259
  324.0 36.0 %all-reduce.2 = (f32[1024]{0:T(1024)}, f32[1024]{0:T(1024)}, f32[12,225]{1,0:T(8,128)}) all-reduce(f32[1024]{0:T(1024)S(1)} %get-tuple-element.77, f32[1024]{0:T(1024)S(1)} %get-tuple-element.78, f32[12,225]{1,0:T(8,128)S(1)} %get-tuple-element.79), channel_id=1, replica_groups=mesh['row'=8,'col'=2,'dp'=2] {'row'}, use_global_device_ids=true, to_apply=%region_14.15 | all-reduce | flops 4748 | bytes 37984 | tf_op jit(solution)/shard_map/psum | solution.py:259
  360.0 22.3 %all-reduce.9.cloned.1.call-done = f32[48,1024]{1,0:T(8,128)} async-done(((f32[48,1024]{1,0:T(8,128)}), f32[48,1024]{1,0:T(8,128)}) %all-reduce.9.cloned.1.call-update) | async-done | bytes 196624 | tf_op jit(solution)/shard_map/psum | solution.py:259
  382.3 23.0 %reduce-scatter.5.cloned.1.call-done = f32[96,256]{1,0:T(8,128)} async-done(((f32[96,1024]{1,0:T(8,128)}), f32[96,256]{1,0:T(8,128)}) %reduce-scatter.5.cloned.1.call-update) | async-done | bytes 98320 | tf_op jit(solution)/shard_map/reduce_scatter | solution.py:230
  405.3 1.6 copy.219
  (87 shorter events, 2.6 us)
Async XLA Ops:
  7.2 50.6 %copy-start = (bf16[48,1024]{1,0:T(8,128)(2,1)S(1)}, bf16[48,1024]{1,0:T(8,128)(2,1)}, u32[]{:S(2)}) copy-start(bf16[48,1024]{1,0:T(8,128)(2,1)} %param.12) | copy-start | bytes 294916
  7.2 46.0 %copy-start.3 = (bf16[1,8,32,1024]{3,2,1,0:T(8,128)(2,1)S(1)}, bf16[1,8,32,1024]{3,2,1,0:T(8,128)(2,1)}, u32[]{:S(2)}) copy-start(bf16[1,8,32,1024]{3,2,1,0:T(8,128)(2,1)} %param.11) | copy-start | bytes 1572868
  7.2 48.2 %copy-start.15 = (bf16[1,3,32,128]{3,2,1,0:T(8,128)(2,1)S(1)}, bf16[1,3,32,128]{3,2,1,0:T(8,128)(2,1)}, u32[]{:S(2)}) copy-start(bf16[1,3,32,128]{3,2,1,0:T(8,128)(2,1)} %param.10) | copy-start | bytes 73732
  7.2 45.9 %all-gather.4.cloned.1.call-start = ((), (), s32[]{:S(2)}) async-start(), calls=%async_computation.2 | async-start | bytes 1327104 | tf_op jit(solution)/shard_map/all_gather | solution.py:184
  7.9 99.5 %all-gather.8.cloned.1.call-start = ((), (), s32[]{:S(2)}) async-start(), calls=%async_computation.6 | async-start | bytes 1769472 | tf_op jit(solution)/shard_map/all_gather | solution.py:218
  21.4 36.4 %copy-start.19 = (f32[1024]{0:T(1024)S(1)}, f32[1024]{0:T(1024)}, u32[]{:S(2)}) copy-start(f32[1024]{0:T(1024)} %param.13) | copy-start | bytes 12292
  21.4 123.4 %all-gather.6.cloned.1.call-start = ((), (), s32[]{:S(2)}) async-start(), calls=%async_computation.3 | async-start | bytes 5898240 | tf_op jit(solution)/shard_map/all_gather | solution.py:186
  53.1 6.1 %copy-start.20 = (s32[1,2]{1,0:T(1,128)S(1)}, s32[1,2]{1,0:T(1,128)}, u32[]{:S(2)}) copy-start(s32[1,2]{1,0:T(1,128)} %param.19) | copy-start | bytes 28
  53.2 9.5 %copy-start.14 = (s32[64,64]{1,0:T(8,128)S(1)}, s32[64,64]{1,0:T(8,128)}, u32[]{:S(2)}) copy-start(s32[64,64]{1,0:T(8,128)} %param.18) | copy-start | bytes 49156
  53.2 10.2 %copy-start.21 = (f32[12,225]{1,0:T(8,128)S(1)}, f32[12,225]{1,0:T(8,128)}, u32[]{:S(2)}) copy-start(f32[12,225]{1,0:T(8,128)} %param.17) | copy-start | bytes 32404
  53.2 178.4 %all-reduce.7.cloned.1.call-start = ((), (), s32[]{:S(2)}) async-start(), calls=%async_computation.7 | async-start | bytes 393216 | tf_op jit(solution)/shard_map/psum | solution.py:259
  53.2 32.7 %collective-permute-start.2 = (bf16[1,8,32,1024]{3,2,1,0:T(8,128)(2,1)S(1)}, bf16[1,8,32,1024]{3,2,1,0:T(8,128)(2,1)S(1)}, u32[]{:S(2)}, u32[]{:S(2)}) collective-permute-start(bf16[1,8,32,1024]{3,2,1,0:T(8,128)(2,1)S(1)} %copy-done.3), channel_id=1, source_target_pairs={{0,28},{4,0},{8,4},{12,8},{16,12},{20,16},{24,20},{28,24},{1,29},{... | collective-permute-start | bytes 1572872 | tf_op jit(solution)/shard_map/ppermute | solution.py:14
  57.8 24.9 %copy-start.10 = (bf16[1,8,32,3,4,4]{2,1,5,4,3,0:T(8,128)(2,1)}, bf16[1,8,32,3,4,4]{2,1,5,4,3,0:T(8,128)(2,1)S(1)}, u32[]{:S(2)}) copy-start(bf16[1,8,32,3,4,4]{2,1,5,4,3,0:T(8,128)(2,1)S(1)} %copy.154) | copy-start | bytes 73732
  58.1 24.4 %collective-permute-start = (bf16[1,8,32,1024]{3,2,1,0:T(8,128)(2,1)S(1)}, bf16[1,8,32,1024]{3,2,1,0:T(8,128)(2,1)S(1)}, u32[]{:S(2)}, u32[]{:S(2)}) collective-permute-start(bf16[1,8,32,1024]{3,2,1,0:T(8,128)(2,1)S(1)} %fusion.11), channel_id=1, source_target_pairs={{0,28},{4,0},{8,4},{12,8},{16,12},{20,16},{24,20},{28,24},{1,29},{... | collective-permute-start | bytes 1572872 | tf_op jit(solution)/shard_map/ppermute | solution.py:14
  62.7 20.0 %copy-start.17 = (s32[4096]{0:T(1024)}, s32[4096]{0:T(1024)S(1)}, u32[]{:S(2)}) copy-start(s32[4096]{0:T(1024)S(1)} %eq.39) | copy-start | bytes 49156
  82.7 4.0 collective-permute-start.1
  86.2 1.5 collective-permute-start.3
  88.1 19.4 %copy-start.5 = (bf16[1,4,8,8,1024]{4,3,2,1,0:T(8,128)(2,1)}, bf16[1,4,8,8,1024]{4,3,2,1,0:T(8,128)(2,1)S(1)}, u32[]{:S(2)}) copy-start(bf16[1,4,8,8,1024]{4,3,2,1,0:T(8,128)(2,1)S(1)} %copy.169) | copy-start | bytes 1572868
  88.1 0.7 copy-start.16
  110.2 34.6 %copy-start.13 = (bf16[256,1024]{1,0:T(8,128)(2,1)S(1)}, bf16[256,1024]{1,0:T(8,128)(2,1)}, u32[]{:S(2)}) copy-start(bf16[256,1024]{1,0:T(8,128)(2,1)} %multiply_convert_fusion.3) | copy-start | bytes 1572868
  151.1 2.6 copy-start.8
  158.5 1.7 copy-start.1
  163.8 2.6 copy-start.2
  170.6 3.0 copy-start.4
  174.2 1.2 copy-start.12
  181.1 4.1 copy-start.11
  181.1 5.1 %copy-start.9 = (bf16[4,64,12,64]{3,2,1,0:T(8,128)(2,1)S(1)}, bf16[4,64,12,64]{3,2,1,0:T(8,128)(2,1)}, u32[]{:S(2)}) copy-start(bf16[4,64,12,64]{3,2,1,0:T(8,128)(2,1)} %reshape.366) | copy-start | bytes 1179652
  181.2 1.6 collective-permute-start.4
  183.0 17.0 %collective-permute-start.5 = (bf16[1,8,32,1024]{3,2,1,0:T(8,128)(2,1)S(1)}, bf16[1,8,32,1024]{3,2,1,0:T(8,128)(2,1)}, u32[]{:S(2)}, u32[]{:S(2)}) collective-permute-start(bf16[1,8,32,1024]{3,2,1,0:T(8,128)(2,1)S(1)} %fusion.25), channel_id=1, source_target_pairs={{0,4},{4,8},{8,12},{12,16},{16,20},{20,24},{24,28},{28,0},{1,5},{5... | collective-permute-start | bytes 1572872 | tf_op jit(solution)/shard_map/ppermute | solution.py:14
  191.9 10.3 %copy-start.6 = (bf16[1,4,8,8,1024]{4,3,2,1,0:T(8,128)(2,1)S(1)}, bf16[1,4,8,8,1024]{4,3,2,1,0:T(8,128)(2,1)}, u32[]{:S(2)}) copy-start(bf16[1,4,8,8,1024]{4,3,2,1,0:T(8,128)(2,1)} %copy-done.5) | copy-start | bytes 1572868
  202.1 107.2 %reduce-scatter.3.cloned.1.call-start = ((), (), s32[]{:S(2)}) async-start(), calls=%async_computation.4 | async-start | bytes 3538944 | tf_op jit(solution)/shard_map/reduce_scatter | solution.py:222
  204.4 105.1 %copy-start.7 = (f32[12,64,64]{1,2,0:T(8,128)S(1)}, f32[12,64,64]{1,2,0:T(8,128)}, u32[]{:S(2)}) copy-start(f32[12,64,64]{1,2,0:T(8,128)} %get-tuple-element.84) | copy-start | bytes 589828
  204.4 105.4 %copy-start.18 = (s32[4096]{0:T(1024)S(1)}, s32[4096]{0:T(1024)}, u32[]{:S(2)}) copy-start(s32[4096]{0:T(1024)} %copy-done.17) | copy-start | bytes 49156
  204.4 177.9 %all-reduce.9.cloned.1.call-start = ((), (), s32[]{:S(2)}) async-start(), calls=%async_computation.8 | async-start | bytes 393216 | tf_op jit(solution)/shard_map/psum | solution.py:259
  231.6 173.7 %reduce-scatter.5.cloned.1.call-start = ((), (), s32[]{:S(2)}) async-start(), calls=%async_computation.5 | async-start | bytes 491520 | tf_op jit(solution)/shard_map/reduce_scatter | solution.py:230
Sparse Core Ops, SparseCore 0:
  10.1 43.0 all-gather.3
  55.3 52.0 all-gather.7
  109.0 35.7 all-gather.5
  202.2 29.2 all-reduce.6
  235.0 74.3 reduce-scatter.2
  312.5 69.7 all-reduce.8
  385.4 19.8 reduce-scatter.4
